TPU v7x, 768 devices: a whole 4x8x12 slice. The times are simulated.
768 devices in a mesh: grp: 96 (over x, y_lo, z), tbl: 8 (over y_hi, core).
Axes of the slice: x: 4, y: 8 (y_hi: 4, y_lo: 2; y = y_hi * 2 + y_lo), z: 12, core: 2. Of those that a mesh axis runs over, the one named last changes fastest.
Arguments:
- next_ids: int32 [98304, 256], P(('grp', 'tbl')), may hold values from 0 to 6143
- next_lengths: int32 [98304, 26], P(('grp', 'tbl')), may hold values from 1 to 8
- slot_of_table: int32 [26], replicated, may hold values from 0 to 31, as said below
- tables: bfloat16 [32, 6144, 128], P('tbl'), may hold values from -2.5 to 2.5
- cross_input: bfloat16 [98304, 3456], P(('grp', 'tbl')), may hold values from -6 to 6
- cotangent: bfloat16 [98304, 3456], P(('grp', 'tbl')), may hold values from -6 to 6
- up_weight: bfloat16 [256, 3456], replicated, may hold values from -0.375 to 0.375
- down_weight: bfloat16 [3456, 256], replicated, may hold values from -0.109375 to 0.109375
Outputs:
- next_embedded: bfloat16 [98304, 3328], P(('grp', 'tbl'))
- grad_up: float32 [256, 3456], P('tbl', 'grp')
- grad_down: float32 [3456, 256], P('grp', 'tbl')
Inputs may be any that keep to these rules, and one draw needn't show every extreme that they name: `next_ids`: entry 8 * s + k of an example's row is the k-th id of the bag held in slot s; entries with k at or past the bag's length, and all entries of slots that hold no table, are padding. `slot_of_table`: distinct slots; owner o along tbl holds slots o * 4 to o * 4 + 3, so an owner holds up to 4 tables and some owner holds exactly 4.
All inputs are finite; a program needn't handle non-finite values.
Results may differ from a plain program's by a relative error of at most 0.0049.
Values may be sent and summed in bfloat16 or wider, within the bound.
A program may use at most 128 MiB of HBM per device.

v0:
```python
import math

import jax
import jax.numpy as jnp
from jax import lax
from jax.sharding import PartitionSpec as P


def split_up(x, dim, count):
    dims = x.shape
    tiles = x.reshape(*dims[:dim], count, dims[dim] // count, *dims[dim + 1 :])
    return jnp.moveaxis(tiles, dim, 0)


def summed_on_arrival(x, axis, dim):
    count = lax.axis_size(axis)
    tiles = lax.all_to_all(split_up(x, dim, count), axis, 0, 0, tiled=True)
    return jnp.sum(tiles, axis=0)


def pool_rows(table_flat, ids, lens, slots, maxlen):
    count = ids.shape[0]
    width = table_flat.shape[1]
    rows_each = table_flat.shape[0] // slots
    ids_three = ids.reshape(count, slots, maxlen)
    offset = lax.broadcasted_iota(jnp.int32, (1, slots, 1), 1) * rows_each
    picked = jnp.take(table_flat, (ids_three + offset).reshape(-1), axis=0).reshape(
        count, slots, maxlen, width
    )
    keep = lax.broadcasted_iota(jnp.int32, (count, slots, maxlen), 2) < lens[:, :, None]
    masked = jnp.where(keep[..., None], picked, jnp.zeros((), picked.dtype))
    pooled = jnp.sum(masked, axis=2, dtype=jnp.float32)
    return pooled.astype(jnp.bfloat16).reshape(count, slots * width)


def on_device(
    next_ids, next_lengths, slot_of_table, tables, cross_input, cotangent, up_weight, down_weight
):
    batch = next_ids.shape[0]
    owners = lax.axis_size("tbl")
    slots = tables.shape[0]
    slots_all = slots * owners
    maxlen = next_ids.shape[1] // slots_all
    width = tables.shape[2]
    feats = slot_of_table.shape[0]
    hit = (slot_of_table[:, None] == lax.broadcasted_iota(jnp.int32, (1, slots_all), 1)).astype(
        jnp.int32
    )
    slot_lengths = jnp.sum(next_lengths[:, :, None] * hit[None, :, :], axis=1)
    block = 64
    items = batch // block
    id_blocks = next_ids.reshape(items, block, slots_all * maxlen)
    len_blocks = slot_lengths.reshape(items, block, slots_all)
    table_flat = tables.reshape(slots * tables.shape[1], width)
    got_ids = lax.all_to_all(id_blocks, "tbl", split_axis=2, concat_axis=1, tiled=True)
    got_lens = lax.all_to_all(len_blocks, "tbl", split_axis=2, concat_axis=1, tiled=True)
    pooled = lax.map(
        lambda pair: pool_rows(table_flat, pair[0], pair[1], slots, maxlen), (got_ids, got_lens)
    )
    returned = lax.all_to_all(pooled, "tbl", split_axis=1, concat_axis=2, tiled=True)
    by_slot = returned.reshape(batch, slots_all, width)
    next_embedded = jnp.take(by_slot, slot_of_table, axis=1).reshape(batch, feats * width)
    low = jnp.dot(cross_input, down_weight, preferred_element_type=jnp.float32).astype(jnp.bfloat16)
    dz = (cotangent.astype(jnp.float32) * cross_input.astype(jnp.float32)).astype(jnp.bfloat16)
    dlow = jnp.dot(dz, up_weight.T, preferred_element_type=jnp.float32).astype(jnp.bfloat16)
    total = batch * lax.axis_size("grp") * owners
    factor = 1.0 / math.sqrt(total)
    part_up = jnp.dot(low.T, dz, preferred_element_type=jnp.float32) * factor
    part_down = jnp.dot(cross_input.T, dlow, preferred_element_type=jnp.float32) * factor
    summed_up, summed_down = (
        lax.psum_scatter(part_up, "grp", scatter_dimension=1, tiled=True),
        lax.psum_scatter(part_down, "grp", scatter_dimension=0, tiled=True),
    )
    grad_up, grad_down = (
        summed_on_arrival(summed_up, "tbl", 0),
        summed_on_arrival(summed_down, "tbl", 1),
    )
    return (next_embedded, grad_up, grad_down)


def solution(mesh):
    return jax.shard_map(
        on_device,
        mesh=mesh,
        in_specs=(
            P(("grp", "tbl"), None),
            P(("grp", "tbl"), None),
            P(),
            P("tbl", None, None),
            P(("grp", "tbl"), None),
            P(("grp", "tbl"), None),
            P(),
            P(),
        ),
        out_specs=(P(("grp", "tbl"), None), P("tbl", "grp"), P("grp", "tbl")),
        check_vma=False,
    )
```

profile of v0, /device:TPU:57, one launch (start us, length us, event | category | flops | bytes accessed | tf_op | source)
XLA Modules:
  0.0 629.8 jit_solution(17401869814721243684)
XLA Ops:
  3.2 7.3 %all-to-all-start = ((s32[8,1,512]{2,1,0:T(1,128)}), s32[8,1,512]{2,1,0:T(1,128)S(1)}, u32[]{:S(2)}, u32[]{:S(2)}) async-start(s32[8,1,512]{2,1,0:T(1,128)} %reshape.155), calls=%async_computation | async-start | bytes 32768 | tf_op jit(solution)/shard_map/all_to_all | solution.py:56
  10.5 5.0 convolution_multiply_fusion.1
  15.5 5.4 fusion.2
  20.9 221.5 %fusion.4 = (f32[256,40]{0,1:T(8,128)S(1)}, f32[40,256]{1,0:T(8,128)S(1)}) fusion(f32[256,3456]{0,1:T(8,128)} %convolution_multiply_fusion.1, f32[3456,256]{1,0:T(8,128)} %fusion.2), kind=kCustom, calls=%all-reduce-scatter.2 | all-reduce-scatter fusion | flops 1966081 | bytes 7163904
  242.5 1.9 collective-permute-start.10
  244.4 1.9 collective-permute-start.11
  246.3 1.9 collective-permute-start.12
  249.3 46.9 %all-to-all-start.1 = ((s32[8,1,4096]{2,1,0:T(1,128)}), s32[8,1,4096]{2,1,0:T(1,128)S(1)}, u32[]{:S(2)}, u32[]{:S(2)}) async-start(s32[8,1,4096]{2,1,0:T(1,128)} %reshape.157), calls=%async_computation.1 | async-start | bytes 262144 | tf_op jit(solution)/shard_map/all_to_all | solution.py:55
  296.3 1.9 collective-permute-start.13
  298.2 1.9 collective-permute-start.19
  300.1 20.1 %collective-permute-done.19 = f32[20,256]{1,0:T(8,128)S(1)} collective-permute-done((f32[20,256]{1,0:T(8,128)S(1)}, f32[20,256]{1,0:T(8,128)S(1)}, u32[]{:S(2)}, u32[]{:S(2)}) %collective-permute-start.19) | collective-permute-done | bytes 20512
  320.2 1.9 collective-permute-start.14
  322.1 1.9 collective-permute-start.15
  324.1 1.9 collective-permute-start.16
  326.0 5.2 collective-permute-start.17
  331.2 1.9 collective-permute-start.18
  333.1 2.8 collective-permute-start
  335.9 1.9 collective-permute-start.1
  338.4 6.6 %collective-permute-start.2 = (f32[256,40]{0,1:T(8,128)S(1)}, f32[256,40]{0,1:T(8,128)S(1)}, u32[]{:S(2)}, u32[]{:S(2)}) collective-permute-start(f32[256,40]{0,1:T(8,128)S(1)} %get-tuple-element.108), channel_id=1, source_target_pairs={{0,24},{8,32},{16,40},{24,48},{32,56},{40,64},{48,72},{56,80},{64,... | collective-permute-start | bytes 122888
  345.0 1.9 collective-permute-start.3
  347.0 14.6 %collective-permute-start.9 = (f32[256,20]{0,1:T(8,128)S(1)}, f32[256,20]{0,1:T(8,128)}, u32[]{:S(2)}, u32[]{:S(2)}) collective-permute-start(f32[256,20]{0,1:T(8,128)S(1)} %slice.4), channel_id=1, source_target_pairs={{0,80},{8,88},{16,96},{24,104},{32,112},{40,120},{48,128},{56,136}... | collective-permute-start | bytes 61448
  361.6 1.3 dynamic-slice.6
  365.1 2.8 concatenate.1
  367.9 16.0 %collective-permute-start.4 = (f32[256,40]{0,1:T(8,128)S(1)}, f32[256,40]{0,1:T(8,128)S(1)}, u32[]{:S(2)}, u32[]{:S(2)}) collective-permute-start(f32[256,40]{0,1:T(8,128)S(1)} %get-tuple-element.108), channel_id=1, source_target_pairs={{0,40},{8,48},{16,56},{24,64},{32,72},{40,80},{48,88},{56,96},{64,... | collective-permute-start | bytes 122888
  383.9 8.3 %collective-permute-start.5 = (f32[256,40]{0,1:T(8,128)S(1)}, f32[256,40]{0,1:T(8,128)S(1)}, u32[]{:S(2)}, u32[]{:S(2)}) collective-permute-start(f32[256,40]{0,1:T(8,128)S(1)} %get-tuple-element.108), channel_id=1, source_target_pairs={{0,48},{8,56},{16,64},{24,72},{32,80},{40,88},{48,96},{56,104},{64... | collective-permute-start | bytes 122888
  392.2 9.0 %collective-permute-start.6 = (f32[256,40]{0,1:T(8,128)S(1)}, f32[256,40]{0,1:T(8,128)S(1)}, u32[]{:S(2)}, u32[]{:S(2)}) collective-permute-start(f32[256,40]{0,1:T(8,128)S(1)} %get-tuple-element.108), channel_id=1, source_target_pairs={{0,56},{8,64},{16,72},{24,80},{32,88},{40,96},{48,104},{56,112},{6... | collective-permute-start | bytes 122888
  401.3 2.0 collective-permute-start.7
  403.3 3.4 collective-permute-start.8
  407.7 4.0 collective-permute-done.7
  411.7 3.4 concatenate
  415.2 13.5 %all-to-all-start.4 = ((f32[8,1,1152]{2,1,0:T(1,128)}), f32[8,1,1152]{2,1,0:T(1,128)S(1)}, u32[]{:S(2)}, u32[]{:S(2)}) async-start(f32[8,1,1152]{2,1,0:T(1,128)} %reshape.161), calls=%async_computation.4 | async-start | bytes 73728 | tf_op jit(solution)/shard_map/all_to_all | solution.py:17
  432.9 7.7 %all-to-all-start.3 = ((f32[8,1,1152]{2,1,0:T(1,128)}), f32[8,1,1152]{2,1,0:T(1,128)}, u32[]{:S(2)}, u32[]{:S(2)}) async-start(f32[8,1,1152]{2,1,0:T(1,128)} %reshape.159), calls=%async_computation.3 | async-start | bytes 73728 | tf_op jit(solution)/shard_map/all_to_all | solution.py:17
  440.5 143.2 %while.12 = (s32[]{:T(128)}, bf16[2,512,512]{2,1,0:T(8,128)(2,1)}, s32[2,512,4]{2,1,0:T(8,128)S(1)}, s32[2,512,32]{1,2,0:T(8,128)}, bf16[24576,128]{1,0:T(8,128)(2,1)}, /*index=5*/s32[]{:T(128)}) while((s32[]{:T(128)}, bf16[2,512,512]{2,1,0:T(8,128)(2,1)}, s32[2,512,4]{2,1,0:T(8,128)S(1)}, s32[2,512,32]{1,2,0:T(8,128)}, ...), condition=%wide.region_3.4_spmd, body=%wide.region_1.3_spmd.sunk | while | flops 6242310 | bytes 16310909 | solution.py:57
  443.3 59.0 %gather_fusion = bf16[16384,128]{1,0:T(8,128)(2,1)} fusion(bf16[24576,128]{1,0:T(8,128)(2,1)} %get-tuple-element.163, s32[16384]{0:T(1024)S(1)} %broadcast_clamp_fusion.2), kind=kCustom, calls=%fused_computation.clone.1 | custom fusion | bytes 8454144 | tf_op jit(solution)/shard_map/while/body/eval_jaxpr/jit(_take)/gather | solution.py:27
  502.7 1.4 iota_compare_fusion.3
  504.1 7.0 %select_reduce_fusion.2 = bf16[512,4,128]{2,1,0:T(4,128)(2,1)S(1)} fusion(pred[512,4,8]{2,1,0:T(4,128)(4,1)S(1)} %copy.89, pred[512,4,8]{2,1,0:T(4,128)(4,1)S(1)} %iota_compare_fusion.3, bf16[16384,128]{1,0:T(8,128)(2,1)} %gather_fusion), kind=kLoop, calls=%fused_computation.2.clone.1 | loop fusion | flops 6029312 | bytes 4751360 | tf_op jit(solution)/shard_map/while/body/eval_jaxpr/reduce_sum | solution.py:32
  514.9 59.0 %gather_fusion = bf16[16384,128]{1,0:T(8,128)(2,1)} fusion(bf16[24576,128]{1,0:T(8,128)(2,1)} %get-tuple-element.163, s32[16384]{0:T(1024)S(1)} %broadcast_clamp_fusion.2), kind=kCustom, calls=%fused_computation.clone.1 | custom fusion | bytes 8454144 | tf_op jit(solution)/shard_map/while/body/eval_jaxpr/jit(_take)/gather | solution.py:27
  574.3 1.4 iota_compare_fusion.3
  575.6 7.0 %select_reduce_fusion.2 = bf16[512,4,128]{2,1,0:T(4,128)(2,1)S(1)} fusion(pred[512,4,8]{2,1,0:T(4,128)(4,1)S(1)} %copy.89, pred[512,4,8]{2,1,0:T(4,128)(4,1)S(1)} %iota_compare_fusion.3, bf16[16384,128]{1,0:T(8,128)(2,1)} %gather_fusion), kind=kLoop, calls=%fused_computation.2.clone.1 | loop fusion | flops 6029312 | bytes 4751360 | tf_op jit(solution)/shard_map/while/body/eval_jaxpr/reduce_sum | solution.py:32
  583.7 3.3 copy.67
  587.0 7.2 %all-to-all-start.2 = ((bf16[2,512,512]{2,0,1:T(2,128)(2,1)}), bf16[2,512,512]{2,0,1:T(2,128)(2,1)S(1)}, u32[]{:S(2)}, u32[]{:S(2)}) async-start(bf16[2,512,512]{2,0,1:T(2,128)(2,1)} %copy.67), calls=%async_computation.2 | async-start | bytes 2097152 | tf_op jit(solution)/shard_map/all_to_all | solution.py:60
  595.7 1.5 reduce.6
  598.7 21.0 %all-to-all-done.2 = bf16[2,512,512]{2,0,1:T(2,128)(2,1)S(1)} async-done(((bf16[2,512,512]{2,0,1:T(2,128)(2,1)}), bf16[2,512,512]{2,0,1:T(2,128)(2,1)S(1)}, u32[]{:S(2)}, u32[]{:S(2)}) %all-to-all-start.2) | async-done | bytes 1048608 | tf_op jit(solution)/shard_map/all_to_all | solution.py:60
  619.6 1.6 copy.86
  621.2 1.7 reshape.133
  622.9 1.4 copy.69
  624.3 1.9 gather_fusion.1
  626.9 1.7 bitcast_select_fusion
  (100 shorter events, 24.0 us)
Async XLA Ops:
  0.6 9.8 %copy-start = (bf16[3456,256]{1,0:T(8,128)(2,1)S(1)}, bf16[3456,256]{1,0:T(8,128)(2,1)}, u32[]{:S(2)}) copy-start(bf16[3456,256]{1,0:T(8,128)(2,1)} %param.17) | copy-start | bytes 5308420
  3.2 246.1 %all-to-all-start = ((s32[8,1,512]{2,1,0:T(1,128)}), s32[8,1,512]{2,1,0:T(1,128)S(1)}, u32[]{:S(2)}, u32[]{:S(2)}) async-start(s32[8,1,512]{2,1,0:T(1,128)} %reshape.155), calls=%async_computation | async-start | bytes 32768 | tf_op jit(solution)/shard_map/all_to_all | solution.py:56
  10.5 5.1 copy-start.1
  10.5 5.1 copy-start.2
  20.9 227.3 %copy-start.3 = (s32[128,256]{1,0:T(8,128)S(1)}, s32[128,256]{1,0:T(8,128)}, u32[]{:S(2)}) copy-start(s32[128,256]{1,0:T(8,128)} %param.10) | copy-start | bytes 393220
  242.5 79.7 %collective-permute-start.10 = (f32[40,256]{1,0:T(8,128)S(1)}, f32[40,256]{1,0:T(8,128)S(1)}, u32[]{:S(2)}, u32[]{:S(2)}) collective-permute-start(f32[40,256]{1,0:T(8,128)S(1)} %get-tuple-element.109), channel_id=1, source_target_pairs={{0,8},{8,16},{16,24},{24,32},{32,40},{40,48},{48,56},{56,64},{64,7... | collective-permute-start | bytes 122888
  244.4 79.7 %collective-permute-start.11 = (f32[40,256]{1,0:T(8,128)S(1)}, f32[40,256]{1,0:T(8,128)S(1)}, u32[]{:S(2)}, u32[]{:S(2)}) collective-permute-start(f32[40,256]{1,0:T(8,128)S(1)} %get-tuple-element.109), channel_id=1, source_target_pairs={{0,16},{8,24},{16,32},{24,40},{32,48},{40,56},{48,64},{56,72},{64,... | collective-permute-start | bytes 122888
  246.3 79.7 %collective-permute-start.12 = (f32[40,256]{1,0:T(8,128)S(1)}, f32[40,256]{1,0:T(8,128)S(1)}, u32[]{:S(2)}, u32[]{:S(2)}) collective-permute-start(f32[40,256]{1,0:T(8,128)S(1)} %get-tuple-element.109), channel_id=1, source_target_pairs={{0,24},{8,32},{16,40},{24,48},{32,56},{40,64},{48,72},{56,80},{64,... | collective-permute-start | bytes 122888
  249.3 165.8 %all-to-all-start.1 = ((s32[8,1,4096]{2,1,0:T(1,128)}), s32[8,1,4096]{2,1,0:T(1,128)S(1)}, u32[]{:S(2)}, u32[]{:S(2)}) async-start(s32[8,1,4096]{2,1,0:T(1,128)} %reshape.157), calls=%async_computation.1 | async-start | bytes 262144 | tf_op jit(solution)/shard_map/all_to_all | solution.py:55
  296.3 34.9 %collective-permute-start.13 = (f32[40,256]{1,0:T(8,128)S(1)}, f32[40,256]{1,0:T(8,128)S(1)}, u32[]{:S(2)}, u32[]{:S(2)}) collective-permute-start(f32[40,256]{1,0:T(8,128)S(1)} %get-tuple-element.109), channel_id=1, source_target_pairs={{0,32},{8,40},{16,48},{24,56},{32,64},{40,72},{48,80},{56,88},{64,... | collective-permute-start | bytes 122888
  298.2 22.0 %collective-permute-start.19 = (f32[20,256]{1,0:T(8,128)S(1)}, f32[20,256]{1,0:T(8,128)S(1)}, u32[]{:S(2)}, u32[]{:S(2)}) collective-permute-start(f32[20,256]{1,0:T(8,128)S(1)} %slice.5), channel_id=1, source_target_pairs={{0,80},{8,88},{16,96},{24,104},{32,112},{40,120},{48,128},{56,136}... | collective-permute-start | bytes 61448
  320.2 43.3 %copy-start.6 = (f32[20,256]{1,0:T(8,128)}, f32[20,256]{1,0:T(8,128)S(1)}, u32[]{:S(2)}) copy-start(f32[20,256]{1,0:T(8,128)S(1)} %collective-permute-done.19) | copy-start | bytes 61444
  320.2 12.9 %collective-permute-start.14 = (f32[40,256]{1,0:T(8,128)S(1)}, f32[40,256]{1,0:T(8,128)S(1)}, u32[]{:S(2)}, u32[]{:S(2)}) collective-permute-start(f32[40,256]{1,0:T(8,128)S(1)} %get-tuple-element.109), channel_id=1, source_target_pairs={{0,40},{8,48},{16,56},{24,64},{32,72},{40,80},{48,88},{56,96},{64,... | collective-permute-start | bytes 122888
  322.1 13.8 %collective-permute-start.15 = (f32[40,256]{1,0:T(8,128)S(1)}, f32[40,256]{1,0:T(8,128)S(1)}, u32[]{:S(2)}, u32[]{:S(2)}) collective-permute-start(f32[40,256]{1,0:T(8,128)S(1)} %get-tuple-element.109), channel_id=1, source_target_pairs={{0,48},{8,56},{16,64},{24,72},{32,80},{40,88},{48,96},{56,104},{64... | collective-permute-start | bytes 122888
  324.1 14.3 %collective-permute-start.16 = (f32[40,256]{1,0:T(8,128)S(1)}, f32[40,256]{1,0:T(8,128)S(1)}, u32[]{:S(2)}, u32[]{:S(2)}) collective-permute-start(f32[40,256]{1,0:T(8,128)S(1)} %get-tuple-element.109), channel_id=1, source_target_pairs={{0,56},{8,64},{16,72},{24,80},{32,88},{40,96},{48,104},{56,112},{6... | collective-permute-start | bytes 122888
  326.0 19.0 %collective-permute-start.17 = (f32[40,256]{1,0:T(8,128)S(1)}, f32[40,256]{1,0:T(8,128)S(1)}, u32[]{:S(2)}, u32[]{:S(2)}) collective-permute-start(f32[40,256]{1,0:T(8,128)S(1)} %get-tuple-element.109), channel_id=1, source_target_pairs={{0,64},{8,72},{16,80},{24,88},{32,96},{40,104},{48,112},{56,120},{... | collective-permute-start | bytes 122888
  331.2 15.8 %collective-permute-start.18 = (f32[40,256]{1,0:T(8,128)S(1)}, f32[40,256]{1,0:T(8,128)S(1)}, u32[]{:S(2)}, u32[]{:S(2)}) collective-permute-start(f32[40,256]{1,0:T(8,128)S(1)} %get-tuple-element.109), channel_id=1, source_target_pairs={{0,72},{8,80},{16,88},{24,96},{32,104},{40,112},{48,120},{56,128},... | collective-permute-start | bytes 122888
  333.1 50.8 %collective-permute-start = (f32[256,40]{0,1:T(8,128)S(1)}, f32[256,40]{0,1:T(8,128)S(1)}, u32[]{:S(2)}, u32[]{:S(2)}) collective-permute-start(f32[256,40]{0,1:T(8,128)S(1)} %get-tuple-element.108), channel_id=1, source_target_pairs={{0,8},{8,16},{16,24},{24,32},{32,40},{40,48},{48,56},{56,64},{64,7... | collective-permute-start | bytes 122888
  335.9 56.3 %collective-permute-start.1 = (f32[256,40]{0,1:T(8,128)S(1)}, f32[256,40]{0,1:T(8,128)S(1)}, u32[]{:S(2)}, u32[]{:S(2)}) collective-permute-start(f32[256,40]{0,1:T(8,128)S(1)} %get-tuple-element.108), channel_id=1, source_target_pairs={{0,16},{8,24},{16,32},{24,40},{32,48},{40,56},{48,64},{56,72},{64,... | collective-permute-start | bytes 122888
  338.4 62.9 %collective-permute-start.2 = (f32[256,40]{0,1:T(8,128)S(1)}, f32[256,40]{0,1:T(8,128)S(1)}, u32[]{:S(2)}, u32[]{:S(2)}) collective-permute-start(f32[256,40]{0,1:T(8,128)S(1)} %get-tuple-element.108), channel_id=1, source_target_pairs={{0,24},{8,32},{16,40},{24,48},{32,56},{40,64},{48,72},{56,80},{64,... | collective-permute-start | bytes 122888
  345.0 58.2 %collective-permute-start.3 = (f32[256,40]{0,1:T(8,128)S(1)}, f32[256,40]{0,1:T(8,128)S(1)}, u32[]{:S(2)}, u32[]{:S(2)}) collective-permute-start(f32[256,40]{0,1:T(8,128)S(1)} %get-tuple-element.108), channel_id=1, source_target_pairs={{0,32},{8,40},{16,48},{24,56},{32,64},{40,72},{48,80},{56,88},{64,... | collective-permute-start | bytes 122888
  347.0 17.8 %copy-start.5 = (f32[40,256]{1,0:T(8,128)}, f32[40,256]{1,0:T(8,128)S(1)}, u32[]{:S(2)}) copy-start(f32[40,256]{1,0:T(8,128)S(1)} %collective-permute-done.18) | copy-start | bytes 122884
  347.0 20.9 %collective-permute-start.9 = (f32[256,20]{0,1:T(8,128)S(1)}, f32[256,20]{0,1:T(8,128)}, u32[]{:S(2)}, u32[]{:S(2)}) collective-permute-start(f32[256,20]{0,1:T(8,128)S(1)} %slice.4), channel_id=1, source_target_pairs={{0,80},{8,88},{16,96},{24,104},{32,112},{40,120},{48,128},{56,136}... | collective-permute-start | bytes 61448
  367.9 39.8 %collective-permute-start.4 = (f32[256,40]{0,1:T(8,128)S(1)}, f32[256,40]{0,1:T(8,128)S(1)}, u32[]{:S(2)}, u32[]{:S(2)}) collective-permute-start(f32[256,40]{0,1:T(8,128)S(1)} %get-tuple-element.108), channel_id=1, source_target_pairs={{0,40},{8,48},{16,56},{24,64},{32,72},{40,80},{48,88},{56,96},{64,... | collective-permute-start | bytes 122888
  383.9 23.7 %collective-permute-start.5 = (f32[256,40]{0,1:T(8,128)S(1)}, f32[256,40]{0,1:T(8,128)S(1)}, u32[]{:S(2)}, u32[]{:S(2)}) collective-permute-start(f32[256,40]{0,1:T(8,128)S(1)} %get-tuple-element.108), channel_id=1, source_target_pairs={{0,48},{8,56},{16,64},{24,72},{32,80},{40,88},{48,96},{56,104},{64... | collective-permute-start | bytes 122888
  392.2 15.5 %collective-permute-start.6 = (f32[256,40]{0,1:T(8,128)S(1)}, f32[256,40]{0,1:T(8,128)S(1)}, u32[]{:S(2)}, u32[]{:S(2)}) collective-permute-start(f32[256,40]{0,1:T(8,128)S(1)} %get-tuple-element.108), channel_id=1, source_target_pairs={{0,56},{8,64},{16,72},{24,80},{32,88},{40,96},{48,104},{56,112},{6... | collective-permute-start | bytes 122888
  401.3 10.4 %collective-permute-start.7 = (f32[256,40]{0,1:T(8,128)S(1)}, f32[256,40]{0,1:T(8,128)S(1)}, u32[]{:S(2)}, u32[]{:S(2)}) collective-permute-start(f32[256,40]{0,1:T(8,128)S(1)} %get-tuple-element.108), channel_id=1, source_target_pairs={{0,64},{8,72},{16,80},{24,88},{32,96},{40,104},{48,112},{56,120},{... | collective-permute-start | bytes 122888
  403.2 3.4 copy-start.4
  403.3 8.4 %collective-permute-start.8 = (f32[256,40]{0,1:T(8,128)S(1)}, f32[256,40]{0,1:T(8,128)}, u32[]{:S(2)}, u32[]{:S(2)}) collective-permute-start(f32[256,40]{0,1:T(8,128)S(1)} %get-tuple-element.108), channel_id=1, source_target_pairs={{0,72},{8,80},{16,88},{24,96},{32,104},{40,112},{48,120},{56,128},... | collective-permute-start | bytes 122888
  415.2 17.7 %all-to-all-start.4 = ((f32[8,1,1152]{2,1,0:T(1,128)}), f32[8,1,1152]{2,1,0:T(1,128)S(1)}, u32[]{:S(2)}, u32[]{:S(2)}) async-start(f32[8,1,1152]{2,1,0:T(1,128)} %reshape.161), calls=%async_computation.4 | async-start | bytes 73728 | tf_op jit(solution)/shard_map/all_to_all | solution.py:17
  432.9 154.2 %all-to-all-start.3 = ((f32[8,1,1152]{2,1,0:T(1,128)}), f32[8,1,1152]{2,1,0:T(1,128)}, u32[]{:S(2)}, u32[]{:S(2)}) async-start(f32[8,1,1152]{2,1,0:T(1,128)} %reshape.159), calls=%async_computation.3 | async-start | bytes 73728 | tf_op jit(solution)/shard_map/all_to_all | solution.py:17
  583.7 10.5 %copy-start.7 = (s32[26]{0:T(128)S(1)}, s32[26]{0:T(128)}, u32[]{:S(2)}) copy-start(s32[26]{0:T(128)} %param.12) | copy-start | bytes 316
  587.0 32.6 %all-to-all-start.2 = ((bf16[2,512,512]{2,0,1:T(2,128)(2,1)}), bf16[2,512,512]{2,0,1:T(2,128)(2,1)S(1)}, u32[]{:S(2)}, u32[]{:S(2)}) async-start(bf16[2,512,512]{2,0,1:T(2,128)(2,1)} %copy.67), calls=%async_computation.2 | async-start | bytes 2097152 | tf_op jit(solution)/shard_map/all_to_all | solution.py:60
where the time goes:
time: 632 us; the launch traced here: 630 us
  blocking collectives  222 us (35%)
  starting transfers between devices  172 us (27%)
  local copies, waits for them, and re-layouts  150 us (24%)
  waiting for transfers between devices  46.8 us (7%)
  other arithmetic  27.4 us (4%)
  matrix products  10.4 us (2%)
    unnamed x1, blocking collectives  222 us
    gather x2, local copies, waits for them, and re-layouts, pool_rows(): jnp.take(table_flat, (ids_three + offset).reshape(-1), axis=0)  118 us
    unnamed x20, starting transfers between devices  88.9 us
    all_to_all x1, starting transfers between devices, on_device(): lax.all_to_all(id_blocks, 'tbl', split_axis=2, concat_axis=1, tiled=True)  46.9 us
    unnamed x20, waiting for transfers between devices  24.7 us
    all_to_all x2, starting transfers between devices, summed_on_arrival(): tiles = lax.all_to_all(split_up(x, dim, count), axis, 0, 0, tiled=True)  21.2 us
    all_to_all x1, waiting for transfers between devices, on_device(): lax.all_to_all(pooled, 'tbl', split_axis=1, concat_axis=2, tiled=True)  21 us
    reduce_sum x2, other arithmetic, pool_rows(): pooled = jnp.sum(masked, axis=2, dtype=jnp.float32)  14.1 us
  transfers between devices with their start and end apart: 25, of which 5 were waited for; matrix products, arithmetic and copies ran while one was open for 63% of the time, Pallas kernels for 0%

commit v1 on v0

v1 whole, which is shorter than its diff:
```python
import functools
import math

import jax
import jax.numpy as jnp
from jax import lax
from jax.experimental import pallas as pl
from jax.experimental.pallas import tpu as pltpu
from jax.sharding import PartitionSpec as P

MESH = pl.DeviceIdType.MESH
F32 = jnp.float32
BF16 = jnp.bfloat16

X, YH, YL, Z = 4, 4, 2, 12
Y = YH * YL
UNROLL = 16
REACH = (0, 2, -1, -3)
SERVE = (6, 7, 2, 3, 4, 5, 1, 0)
FAR = (6, 5, 7, 4, 8, 3, 9, 2, 10, 1, 11)


def kernel(
    ids_hbm,
    lens_ref,
    slot_row_ref,
    slot_ref,
    tables_hbm,
    x_hbm,
    c_hbm,
    up_hbm,
    down_hbm,
    emb_ref,
    gup_ref,
    gdown_ref,
    ids_v,
    words,
    got_words,
    words_s,
    tab_b,
    tab,
    x_v,
    c_v,
    up_v,
    down_v,
    dz_v,
    low_v,
    dlow_v,
    half_out,
    half_in,
    own,
    xs,
    x_relay_in,
    x_direct,
    x_relay_out,
    x_summed,
    sx,
    zs,
    zr,
    ys,
    yr,
    turned,
    bags,
    pooled,
    arrived,
    ld_sem,
    ids_s,
    ids_r,
    pair_s,
    pair_r,
    xa_s,
    xa_r,
    xb_s,
    xb_r,
    xc_s,
    xc_r,
    z_s,
    z_r,
    y_s,
    y_r,
    e_s,
    e_r,
):
    g = lax.axis_index("grp")
    t = lax.axis_index("tbl")
    x, yl, z = g // (YL * Z), (g // Z) % YL, g % Z
    yh, c = t // 2, t % 2
    y = yh * 2 + yl
    sign = 1 - 2 * yl
    rows_flat = tables_hbm.shape[0]
    rows_each = rows_flat // 4
    width = x_hbm.shape[1]
    per_x = width // X
    per_y = per_x // YL
    per_z = per_y // Z
    examples = ids_hbm.shape[0]

    def place(px, py, pz, pc):
        return ((px * YL + py % 2) * Z + pz, (py // 2) * 2 + pc)

    def remote(src, dst, send, recv, where):
        return pltpu.make_async_remote_copy(
            src_ref=src, dst_ref=dst, send_sem=send, recv_sem=recv, device_id=where, device_id_type=MESH
        )

    loads = [
        pltpu.make_async_copy(src, dst, ld_sem.at[i])
        for i, (src, dst) in enumerate(
            (
                (ids_hbm, ids_v),
                (x_hbm, x_v),
                (down_hbm, down_v),
                (c_hbm, c_v),
                (up_hbm, up_v),
                (tables_hbm, tab_b),
            )
        )
    ]
    for load in loads:
        load.start()

    barrier = pltpu.get_barrier_semaphore()
    met = 0
    for dy in range(Y):
        for b in range(2):
            if dy or b:
                pl.semaphore_signal(
                    barrier, inc=1, device_id=place(x, (y + dy) % Y, z, (c + b) % 2), device_id_type=MESH
                )
                met += 1
    for dx in (1, X - 1):
        pl.semaphore_signal(barrier, inc=1, device_id=place((x + dx) % X, y, z, c), device_id_type=MESH)
        met += 1
    for dz in range(1, Z):
        pl.semaphore_signal(barrier, inc=1, device_id=place(x, y, (z + dz) % Z, c), device_id_type=MESH)
        met += 1

    loads[0].wait()
    entries = ids_hbm.shape[1]
    spread = (lax.broadcasted_iota(jnp.int32, (entries, slot_row_ref.shape[1]), 0) // 8 == slot_row_ref[...]).astype(BF16)
    lens = lax.dot_general(
        spread, lens_ref[...].astype(F32).astype(BF16), (((1,), (1,)), ((), ())), preferred_element_type=F32
    )
    entry = lax.broadcasted_iota(jnp.int32, (entries, examples), 0)
    local = jnp.transpose(ids_v[...]) + ((entry // 8) % 4) * rows_each
    local = jnp.where((entry % 8).astype(F32) < lens, local, rows_flat)
    by_owner = local.reshape(8, 2, 16, examples)
    words[...] = by_owner[:, 0] + by_owner[:, 1] * 65536

    pl.semaphore_wait(barrier, met)

    ids_copies = {}
    for r in range(1, 8):
        py, pc = (y + sign * REACH[r // 2] + Y) % Y, (c + r % 2) % 2
        ids_copies[r] = remote(
            words.at[(py // 2) * 2 + pc], got_words.at[r], ids_s.at[r], ids_r.at[r], place(x, py, z, pc)
        )
        ids_copies[r].start()
    to_smem = [
        pltpu.make_async_copy(words.at[t] if r == 0 else got_words.at[r], words_s.at[r], ld_sem.at[6 + r])
        for r in range(8)
    ]
    to_smem[0].start()

    loads[1].wait()
    loads[2].wait()
    col = lax.broadcasted_iota(jnp.int32, (256, 256), 1)
    row = lax.broadcasted_iota(jnp.int32, (256, 256), 0)
    core = jnp.where(col < 128, 1 - c, c)
    order = (row == (((col % 128) // 32) * 2 + core) * 32 + col % 32).astype(BF16)
    low = jnp.dot(x_v[...], down_v[...], preferred_element_type=F32).astype(BF16)
    low_v[...] = jnp.dot(low, order, preferred_element_type=F32).astype(BF16)
    loads[3].wait()
    loads[4].wait()
    dz_v[...] = (c_v[...].astype(F32) * x_v[...].astype(F32)).astype(BF16)
    dlow = lax.dot_general(
        dz_v[...], up_v[...], (((1,), (1,)), ((), ())), preferred_element_type=F32
    ).astype(BF16)
    dlow_v[...] = jnp.dot(dlow, order, preferred_element_type=F32).astype(BF16)

    def partials(i, carry):
        r0 = pl.multiple_of(i * 384, 128)
        for k, (left, right) in enumerate(((dz_v, low_v), (x_v, dlow_v))):
            part = lax.dot_general(
                left[:, pl.ds(r0, 384)], right[...], (((0,), (0,)), ((), ())), preferred_element_type=F32
            )
            half_out[k, pl.ds(r0, 384), :] = part[:, :128].astype(BF16)
            own[k, pl.ds(r0, 384), :] = part[:, 128:]
        return carry

    lax.fori_loop(0, width // 384, partials, 0)

    block = [((x + d) % X) * per_x for d in (2, 1, X - 1, 0)]
    pair = []
    for j in range(4):
        rows = pl.ds(pl.multiple_of(block[j], 16), per_x)
        pair.append(
            remote(
                half_out.at[:, rows], half_in.at[:, rows], pair_s.at[j], pair_r.at[j], place(x, y, z, (c + 1) % 2)
            )
        )
        pair[j].start()

    loads[5].wait()

    def widen(i, carry):
        r0 = pl.multiple_of(i * 256, 256)
        tab[pl.ds(r0, 256), :] = tab_b[pl.ds(r0, 256), :].astype(F32)
        return carry

    lax.fori_loop(0, rows_flat // 256, widen, 0)
    tab[pl.ds(rows_flat, 8), :] = jnp.zeros((8, 128), F32)

    step = 144

    def chip_sum(k, start):
        rows = pl.ds(pl.multiple_of(start, 16), step)
        return own[k, rows, :] + half_in[k, rows, :].astype(F32)

    def stage(j, kinds):
        def body(i, carry):
            for k in kinds:
                start = block[j] + i * step
                xs[k, pl.ds(pl.multiple_of(start, 16), step), :] = chip_sum(k, start).astype(BF16)
            return carry

        lax.fori_loop(0, per_x // step, body, 0)

    ahead, behind = place((x + 1) % X, y, z, c), place((x + X - 1) % X, y, z, c)

    def x_rows(j):
        return pl.ds(pl.multiple_of(block[j], 16), per_x)

    pair[0].wait_recv()
    stage(0, (0, 1))
    relay = [
        remote(xs.at[0, x_rows(0)], x_relay_in.at[0], xa_s.at[0], xa_r.at[0], ahead),
        remote(xs.at[1, x_rows(0)], x_relay_in.at[1], xa_s.at[1], xa_r.at[1], behind),
    ]
    for copy in relay:
        copy.start()
    pair[1].wait_recv()
    stage(1, (1,))
    pair[2].wait_recv()
    stage(2, (0,))
    direct = [
        remote(xs.at[1, x_rows(1)], x_direct.at[1], xb_s.at[0], xb_r.at[0], ahead),
        remote(xs.at[0, x_rows(2)], x_direct.at[0], xb_s.at[1], xb_r.at[1], behind),
    ]
    for copy in direct:
        copy.start()

    for r in range(1, 8):
        ids_copies[r].wait_recv()
        to_smem[r].start()
    for r in range(8):
        to_smem[r].wait()

    def pool(r):
        def body(i, carry):
            a = i // (examples // UNROLL)
            e = (i % (examples // UNROLL)) * UNROLL
            for u in range(UNROLL):
                low_rows, high_rows = [], []
                for k in range(8):
                    word = words_s[r, a * 8 + k, e + u]
                    low_rows.append(tab[pl.ds(word & 0xFFFF, 1), :])
                    high_rows.append(tab[pl.ds(lax.shift_right_logical(word, 16), 1), :])
                for half, picked in enumerate((low_rows, high_rows)):
                    while len(picked) > 1:
                        picked = [picked[n] + picked[n + 1] for n in range(0, len(picked), 2)]
                    bags[half, pl.ds(u, 1), :] = picked[0]
            at = pl.ds(pl.multiple_of(e, UNROLL), UNROLL)
            for half in range(2):
                if r == 0:
                    arrived[t * 4 + a + 2 * half, at, :] = bags[half].astype(BF16)
                else:
                    pooled[r, a + 2 * half, at, :] = bags[half].astype(BF16)
            return carry

        lax.fori_loop(0, 2 * (examples // UNROLL), body, 0)
        if r == 0:
            return None
        py, pc = (y + (-sign if r // 2 == 1 else sign) * (REACH[r // 2]) + 2 * Y) % Y, (c + r % 2) % 2
        copy = remote(
            pooled.at[r], arrived.at[pl.ds(t * 4, 4)], e_s.at[r], e_r.at[r], place(x, py, z, pc)
        )
        copy.start()
        return copy

    sent = [pool(SERVE[0])]

    for copy in relay:
        copy.wait_recv()

    def add_relay(i, carry):
        rows = pl.ds(pl.multiple_of(i * step, 16), step)
        for k in range(2):
            total = chip_sum(k, block[1 + k] + i * step) + x_relay_in[k, rows, :].astype(F32)
            x_relay_out[k, rows, :] = total.astype(BF16)
        return carry

    lax.fori_loop(0, per_x // step, add_relay, 0)
    summed = [
        remote(x_relay_out.at[0], x_summed.at[0], xc_s.at[0], xc_r.at[0], ahead),
        remote(x_relay_out.at[1], x_summed.at[1], xc_s.at[1], xc_r.at[1], behind),
    ]
    for copy in summed:
        copy.start()

    for n in (1, 2):
        sent.append(pool(SERVE[n]))

    pair[3].wait_recv()
    for copy in direct:
        copy.wait_recv()
    for copy in summed:
        copy.wait_recv()

    def add_x(i, carry):
        rows = pl.ds(pl.multiple_of(i * step, 16), step)
        for k in range(2):
            total = chip_sum(k, block[3] + i * step)
            sx[k, rows, :] = total + x_direct[k, rows, :].astype(F32) + x_summed[k, rows, :].astype(F32)
        return carry

    lax.fori_loop(0, per_x // step, add_x, 0)
    spare = jnp.zeros((8, 128), F32)
    for pz in range(Z):
        for k in range(2):
            parts = [sx[k, n * per_y + pz * per_z : n * per_y + (pz + 1) * per_z, :] for n in range(YL)]
            zs[pz, k, :, :] = jnp.concatenate(parts + [spare], axis=0).astype(BF16)
    along_z = []
    for d in FAR:
        pz = (z + d) % Z
        along_z.append(remote(zs.at[pz], zr.at[d - 1], z_s.at[d], z_r.at[d], place(x, y, pz, c)))
        along_z[-1].start()

    for n in (3, 4, 5, 6):
        sent.append(pool(SERVE[n]))

    for copy in along_z:
        copy.wait_recv()
    both = [zs[z, k, :, :].astype(F32) for k in range(2)]
    for d in range(1, Z):
        both = [both[k] + zr[d - 1, k, :, :].astype(F32) for k in range(2)]
    for n in range(YL):
        rows = slice(n * per_z, (n + 1) * per_z)
        ys[n, :, :] = jnp.concatenate([both[0][rows], both[1][rows], spare], axis=0).astype(BF16)
    along_y = []
    for d in (4, 3, 5, 2, 6, 1, 7):
        py = (y + d) % Y
        along_y.append(remote(ys.at[py % 2], yr.at[d - 1], y_s.at[d], y_r.at[d], place(x, py, z, c)))
        along_y[-1].start()

    pool(SERVE[7])

    for copy in along_y:
        copy.wait_recv()
    total = ys[yl, :, :].astype(F32)
    for d in range(1, Y):
        total = total + yr[d - 1, :, :].astype(F32)
    total = total * (1.0 / math.sqrt(examples * X * Y * Z * 2))
    turned[...] = jnp.transpose(jnp.concatenate([total, jnp.zeros((128 - total.shape[0], 128), F32)], axis=0))
    gup_ref[...] = turned[pl.ds(pl.multiple_of(yh * 32, 32), 32), 0:per_z]
    mine = jnp.zeros((per_z, 32), F32)
    for n in range(YH):
        mine = jnp.where(yh == n, total[per_z : 2 * per_z, n * 32 : (n + 1) * 32], mine)
    gdown_ref[...] = mine

    for copy in sent:
        copy.wait_recv()
    for f in range(slot_ref.shape[0]):
        emb_ref[:, f * 128 : (f + 1) * 128] = arrived[slot_ref[f], :, :]

    for copy in [*ids_copies.values(), *pair, *relay, *direct, *summed, *along_z, *along_y, *sent]:
        copy.wait_send()


def on_device(
    next_ids, next_lengths, slot_of_table, tables, cross_input, cotangent, up_weight, down_weight
):
    examples, entries = next_ids.shape
    feats = slot_of_table.shape[0]
    slots, rows_each, embed = tables.shape
    width = cross_input.shape[1]
    rank = up_weight.shape[0]
    per_x = width // X
    per_z = per_x // YL // Z
    whole = pl.BlockSpec(memory_space=pltpu.VMEM)
    anywhere = pl.BlockSpec(memory_space=pl.ANY)
    vmem, dma = pltpu.VMEM, pltpu.SemaphoreType.DMA
    return pl.pallas_call(
        kernel,
        out_shape=(
            jax.ShapeDtypeStruct((examples, feats * embed), BF16),
            jax.ShapeDtypeStruct((32, per_z), F32),
            jax.ShapeDtypeStruct((per_z, 32), F32),
        ),
        in_specs=[
            anywhere,
            whole,
            whole,
            pl.BlockSpec(memory_space=pltpu.SMEM),
            anywhere,
            anywhere,
            anywhere,
            anywhere,
            anywhere,
        ],
        out_specs=(whole, whole, whole),
        scratch_shapes=[
            vmem((examples, entries), jnp.int32),
            vmem((8, 16, examples), jnp.int32),
            vmem((8, 16, examples), jnp.int32),
            pltpu.SMEM((8, 16, examples), jnp.int32),
            vmem((slots * rows_each, embed), BF16),
            vmem((slots * rows_each + 8, embed), F32),
            vmem((examples, width), BF16),
            vmem((examples, width), BF16),
            vmem((rank, width), BF16),
            vmem((width, rank), BF16),
            vmem((examples, width), BF16),
            vmem((examples, rank), BF16),
            vmem((examples, rank), BF16),
            vmem((2, width, 128), BF16),
            vmem((2, width, 128), BF16),
            vmem((2, width, 128), F32),
            vmem((2, width, 128), BF16),
            vmem((2, per_x, 128), BF16),
            vmem((2, per_x, 128), BF16),
            vmem((2, per_x, 128), BF16),
            vmem((2, per_x, 128), BF16),
            vmem((2, per_x, 128), F32),
            vmem((Z, 2, 80, 128), BF16),
            vmem((Z - 1, 2, 80, 128), BF16),
            vmem((YL, 80, 128), BF16),
            vmem((Y - 1, 80, 128), BF16),
            vmem((128, 128), F32),
            vmem((2, UNROLL, embed), F32),
            vmem((8, 4, examples, embed), BF16),
            vmem((32, examples, embed), BF16),
            dma((14,)),
            dma((8,)),
            dma((8,)),
            dma((4,)),
            dma((4,)),
            dma((2,)),
            dma((2,)),
            dma((2,)),
            dma((2,)),
            dma((2,)),
            dma((2,)),
            dma((Z,)),
            dma((Z,)),
            dma((Y,)),
            dma((Y,)),
            dma((8,)),
            dma((8,)),
        ],
        compiler_params=pltpu.CompilerParams(
            collective_id=0, has_side_effects=True, vmem_limit_bytes=60 * 2**20
        ),
    )(
        next_ids,
        next_lengths,
        slot_of_table.reshape(1, feats),
        slot_of_table,
        tables.reshape(slots * rows_each, embed),
        cross_input,
        cotangent,
        up_weight,
        down_weight,
    )


def solution(mesh):
    return jax.shard_map(
        on_device,
        mesh=mesh,
        in_specs=(
            P(("grp", "tbl"), None),
            P(("grp", "tbl"), None),
            P(),
            P("tbl", None, None),
            P(("grp", "tbl"), None),
            P(("grp", "tbl"), None),
            P(),
            P(),
        ),
        out_specs=(P(("grp", "tbl"), None), P("tbl", "grp"), P("grp", "tbl")),
        check_vma=False,
    )
```

time: 632 us -> 83.8 us (0.13)
  the two profiles are of different devices: /device:TPU:57 before, /device:TPU:7 now
where the time goes in v1:
time: 83.8 us; the launch traced here: 83.4 us
  Pallas kernels  76.5 us (91%)
  local copies, waits for them, and re-layouts  6.29 us (8%)
    pallas_call x1, Pallas kernels, on_device(): pl.pallas_call(kernel, out_shape=(jax.ShapeDtypeStruct((examples, feats *...  76.5 us
    unnamed x3, local copies, waits for them, and re-layouts  4.88 us

profile of v1, /device:TPU:7, one launch (start us, length us, event | category | flops | bytes accessed | tf_op | source)
XLA Modules:
  0.0 83.4 jit_solution(6475295063196201235)
XLA Ops:
  0.6 1.4 %copy.11.lens_ref = s32[128,26]{1,0:T(8,128)} copy(s32[128,26]{0,1:T(8,128)} %param.9) | data formatting | bytes 26624 | tf_op args[1]
  2.1 76.5 %shard_map.103 = (bf16[128,3328]{1,0:T(8,128)(2,1)}, f32[32,36]{1,0:T(8,128)}, f32[36,32]{1,0:T(8,128)}) custom-call(s32[128,256]{1,0:T(8,128)} %ids_hbm.1, s32[128,26]{1,0:T(8,128)} %copy.11.lens_ref, s32[1,26]{1,0:T(1,128)} %bitcast.3, s32[26]{0:T(128)} %slot_ref.1, bf16[24576,128]{1,0:T(8,128)(2,1)} %bitcast.2, bf16[128,3456]{1,0:T(8,128)(2,1)} %x_hbm.1, ...), custom_call_target="tpu_custom_call" | custom-call | tf_op jit(solution)/shard_map/pallas_call | solution.py:393
  78.6 1.4 %copy.12 = f32[36,32]{0,1:T(8,128)} copy(f32[36,32]{1,0:T(8,128)} %get-tuple-element.5) | data formatting | bytes 9216 | tf_op jit(solution)/shard_map/pallas_call | solution.py:393
  80.0 2.1 %copy.15 = bf16[128,3328]{1,0:T(8,128)(2,1)} copy(bf16[128,3328]{1,0:T(8,128)(2,1)} %get-tuple-element.9) | data formatting | bytes 1703936
  82.1 1.3 %copy.16 = f32[32,36]{1,0:T(8,128)} copy(f32[32,36]{1,0:T(8,128)} %get-tuple-element.10) | data formatting | bytes 9216

commit v2 on v1

v2 whole, which is shorter than its diff:
```python
import math

import jax
import jax.numpy as jnp
from jax import lax
from jax.experimental import pallas as pl
from jax.experimental.pallas import tpu as pltpu
from jax.sharding import PartitionSpec as P

MESH = pl.DeviceIdType.MESH
F32 = jnp.float32
BF16 = jnp.bfloat16

X, YH, YL, Z = 4, 4, 2, 12
Y = YH * YL
REACH = (0, -1, 2, -3)
FAR = (6, 5, 7, 4, 8, 3, 9, 2, 10, 1, 11)


def kernel(
    ids_hbm,
    lens_hbm,
    slot_row_hbm,
    tables_hbm,
    x_hbm,
    c_hbm,
    up_hbm,
    down_hbm,
    arrived,
    gup_hbm,
    gdown_hbm,
    ids_v,
    lens_v,
    slot_row_v,
    words,
    got_words,
    local_ids,
    window,
    tab_b,
    tab,
    x_v,
    c_v,
    up_v,
    down_v,
    dz_v,
    low_v,
    dlow_v,
    half_out,
    half_in,
    own,
    xs,
    x_relay_in,
    x_direct,
    x_relay_out,
    x_summed,
    sx,
    zs,
    zr,
    ys,
    yr,
    turned,
    gup_v,
    gdown_v,
    bags,
    pooled,
    ld_sem,
    win_sem,
    ids_s,
    ids_r,
    pair_s,
    pair_r,
    xa_s,
    xa_r,
    xb_s,
    xb_r,
    xc_s,
    xc_r,
    z_s,
    z_r,
    y_s,
    y_r,
    e_s,
    e_r,
):
    g = lax.axis_index("grp")
    t = lax.axis_index("tbl")
    x, yl, z = g // (YL * Z), (g // Z) % YL, g % Z
    yh, c = t // 2, t % 2
    y = yh * 2 + yl
    sign = 1 - 2 * yl
    rows_flat = tables_hbm.shape[0]
    rows_each = rows_flat // 4
    width = x_hbm.shape[1]
    per_x = width // X
    per_y = per_x // YL
    per_z = per_y // Z
    examples, entries = ids_hbm.shape

    def place(px, py, pz, pc):
        return ((px * YL + py % 2) * Z + pz, (py // 2) * 2 + pc)

    def remote(src, dst, send, recv, where):
        return pltpu.make_async_remote_copy(
            src_ref=src, dst_ref=dst, send_sem=send, recv_sem=recv, device_id=where, device_id_type=MESH
        )

    loads = [
        pltpu.make_async_copy(src, dst, ld_sem.at[i])
        for i, (src, dst) in enumerate(
            (
                (lens_hbm, lens_v),
                (slot_row_hbm, slot_row_v),
                (ids_hbm, ids_v),
                (x_hbm, x_v),
                (down_hbm, down_v),
                (c_hbm, c_v),
                (up_hbm, up_v),
                (tables_hbm, tab_b),
            )
        )
    ]
    for load in loads:
        load.start()

    barrier = pltpu.get_barrier_semaphore()
    met = 0
    for dy in range(Y):
        for b in range(2):
            if dy or b:
                pl.semaphore_signal(
                    barrier, inc=1, device_id=place(x, (y + dy) % Y, z, (c + b) % 2), device_id_type=MESH
                )
                met += 1
    for dx in (1, X - 1):
        pl.semaphore_signal(barrier, inc=1, device_id=place((x + dx) % X, y, z, c), device_id_type=MESH)
        met += 1
    for dz in range(1, Z):
        pl.semaphore_signal(barrier, inc=1, device_id=place(x, y, (z + dz) % Z, c), device_id_type=MESH)
        met += 1

    loads[3].wait()
    loads[4].wait()
    col = lax.broadcasted_iota(jnp.int32, (256, 256), 1)
    row = lax.broadcasted_iota(jnp.int32, (256, 256), 0)
    core = jnp.where(col < 128, 1 - c, c)
    order = (row == (((col % 128) // 32) * 2 + core) * 32 + col % 32).astype(BF16)
    low = jnp.dot(x_v[...], down_v[...], preferred_element_type=F32).astype(BF16)
    low_v[...] = jnp.dot(low, order, preferred_element_type=F32).astype(BF16)
    loads[5].wait()
    loads[6].wait()
    dz_v[...] = (c_v[...].astype(F32) * x_v[...].astype(F32)).astype(BF16)
    dlow = lax.dot_general(
        dz_v[...], up_v[...], (((1,), (1,)), ((), ())), preferred_element_type=F32
    ).astype(BF16)
    dlow_v[...] = jnp.dot(dlow, order, preferred_element_type=F32).astype(BF16)

    pl.semaphore_wait(barrier, met)
    for n in range(3):
        loads[n].wait()
    spread = (lax.broadcasted_iota(jnp.int32, (entries, slot_row_v.shape[1]), 0) // 8 == slot_row_v[...]).astype(BF16)
    lens = lax.dot_general(
        spread, lens_v[...].astype(F32).astype(BF16), (((1,), (0,)), ((), ())), preferred_element_type=F32
    )
    entry = lax.broadcasted_iota(jnp.int32, (entries, examples), 0)
    local = jnp.transpose(ids_v[...]) + ((entry // 8) % 4) * rows_each
    local = jnp.where((entry % 8).astype(F32) < lens, local, rows_flat)
    by_owner = local.reshape(8, 2, 16, examples)
    words[...] = by_owner[:, 0] + by_owner[:, 1] * 65536

    def ids_copy(r):
        py, pc = (y + sign * REACH[r // 2] + Y) % Y, (c + r % 2) % 2
        return remote(words.at[(py // 2) * 2 + pc], got_words.at[r], ids_s.at[r], ids_r.at[r], place(x, py, z, pc))

    for r in range(7, 0, -1):
        ids_copy(r).start()

    step = 144

    def chip_sum(k, start):
        rows = pl.ds(pl.multiple_of(start, 16), step)
        return own[k, rows, :] + half_in[k, rows, :].astype(F32)

    def stage(j, q, k):
        def body(i, carry):
            start = first_row(j, q) + i * step
            xs[k, pl.ds(pl.multiple_of(start, 16), step), :] = chip_sum(k, start).astype(BF16)
            return carry

        lax.fori_loop(0, per_y // step, body, 0)

    ahead, behind = place((x + 1) % X, y, z, c), place((x + X - 1) % X, y, z, c)

    def relay(q, k):
        n = 2 * q + k
        where = (ahead, behind)[k]
        return remote(xs.at[k, rows_of(0, q)], x_relay_in.at[q, k], xa_s.at[n], xa_r.at[n], where)

    def direct(q, k):
        n = 2 * q + k
        where = (behind, ahead)[k]
        return remote(xs.at[k, rows_of(2 - k, q)], x_direct.at[q, k], xb_s.at[n], xb_r.at[n], where)

    def summed(q, k):
        n = 2 * q + k
        where = (ahead, behind)[k]
        return remote(x_relay_out.at[q, k], x_summed.at[q, k], xc_s.at[n], xc_r.at[n], where)

    def along_z(q, d):
        pz, n = (z + d) % Z, q * Z + d
        return remote(zs.at[q, pz], zr.at[q, d - 1], z_s.at[n], z_r.at[n], place(x, y, pz, c))

    def along_y(d):
        return remote(ys.at[d % 2], yr.at[d - 1], y_s.at[d], y_r.at[d], place(x, (y + d) % Y, z, c))

    def x_relay(q):
        pair(0, q).wait_recv()
        for k in range(2):
            stage(0, q, k)
            relay(q, k).start()

    def x_near(q):
        for k in range(2):
            pair(2 - k, q).wait_recv()
            stage(2 - k, q, k)
            direct(q, k).start()

    def x_forward(q):
        for k in range(2):
            relay(q, k).wait_recv()

            def body(i, carry, k=k):
                rows = pl.ds(pl.multiple_of(i * step, 16), step)
                total = chip_sum(k, first_row(1 + k, q) + i * step) + x_relay_in[q, k, rows, :].astype(F32)
                x_relay_out[q, k, rows, :] = total.astype(BF16)
                return carry

            lax.fori_loop(0, per_y // step, body, 0)
            summed(q, k).start()

    def z_send(q):
        pair(3, q).wait_recv()
        for k in range(2):
            direct(q, k).wait_recv()
            summed(q, k).wait_recv()

        def body(i, carry):
            rows = pl.ds(pl.multiple_of(i * step, 16), step)
            for k in range(2):
                total = chip_sum(k, first_row(3, q) + i * step)
                total = total + x_direct[q, k, rows, :].astype(F32) + x_summed[q, k, rows, :].astype(F32)
                sx[k, rows, :] = total
            return carry

        lax.fori_loop(0, per_y // step, body, 0)
        spare = jnp.zeros((8, 128), F32)
        for pz in range(Z):
            parts = [sx[k, pz * per_z : (pz + 1) * per_z, :] for k in range(2)]
            zs[q, pz, :, :] = jnp.concatenate(parts + [spare], axis=0).astype(BF16)
        for d in FAR:
            along_z(q, d).start()

    def y_send(q):
        total = zs[q, z, :, :].astype(F32)
        for d in FAR:
            along_z(q, d).wait_recv()
            total = total + zr[q, d - 1, :, :].astype(F32)
        ys[q, :, :] = total.astype(BF16)
        for d in ((4, 2, 6), (3, 5, 1, 7))[q]:
            along_y(d).start()

    tiles = width // 384
    first_tile = ((x + 2) % X) * per_x // 384

    def partials(i, carry):
        r0 = pl.multiple_of(((i + first_tile) % tiles) * 384, 128)
        for k, (left, right) in enumerate(((dz_v, low_v), (x_v, dlow_v))):
            part = lax.dot_general(
                left[:, pl.ds(r0, 384)], right[...], (((0,), (0,)), ((), ())), preferred_element_type=F32
            )
            half_out[k, pl.ds(r0, 384), :] = part[:, :128].astype(BF16)
            own[k, pl.ds(r0, 384), :] = part[:, 128:]
        return carry

    part_of = [yl, 1 - yl]

    def first_row(j, q):
        return ((x + (2, 1, X - 1, 0)[j]) % X) * per_x + part_of[q] * per_y

    def rows_of(j, q):
        return pl.ds(pl.multiple_of(first_row(j, q), 16), per_y)

    def pair(j, q):
        rows, n = rows_of(j, q), 2 * j + q
        return remote(
            half_out.at[:, rows], half_in.at[:, rows], pair_s.at[n], pair_r.at[n], place(x, y, z, (c + 1) % 2)
        )

    lax.fori_loop(0, tiles // 3, partials, 0)
    pair(0, 0).start()
    lax.fori_loop(tiles // 3, 2 * tiles // 3, partials, 0)
    pair(2, 0).start()
    lax.fori_loop(2 * tiles // 3, tiles, partials, 0)
    for j, q in ((1, 0), (0, 1), (1, 1), (2, 1), (3, 0), (3, 1)):
        pair(j, q).start()

    x_relay(0)
    loads[7].wait()

    def widen(i, carry):
        r0 = pl.multiple_of(i * 256, 256)
        tab[pl.ds(r0, 256), :] = tab_b[pl.ds(r0, 256), :].astype(F32)
        return carry

    lax.fori_loop(0, rows_flat // 256, widen, 0)
    tab[pl.ds(rows_flat, 8), :] = jnp.zeros((8, 128), F32)

    x_near(0)

    local_words = [words[t]]
    for r in range(1, 8):
        ids_copy(r).wait_recv()
        local_words.append(got_words[r])
    for r in range(8):
        pair_of = local_words[r].reshape(2, 8, examples)
        local_ids[r, 0:2] = pair_of & 0xFFFF
        local_ids[r, 2:4] = lax.shift_right_logical(pair_of, 16)

    def refill(r, slot, s):
        return pltpu.make_async_copy(local_ids.at[r, slot], window.at[s], win_sem.at[s])

    def partner(n):
        far, other = 3 - n // 2, (n + n // 6) % 2
        return 2 * far + other, far, other

    def bags_to(n):
        r, far, other = partner(n)
        where = place(x, (y - sign * far + Y) % Y, z, (c + other) % 2)
        return remote(pooled.at[r], arrived.at[pl.ds(t * 4, 4)], e_s.at[r], e_r.at[r], where)

    for s in range(2):
        refill(partner(0)[0], s, s).start()

    events = {2: [(x_forward, 0), (x_relay, 1), (x_near, 1)], 6: [(z_send, 0)], 8: [(x_forward, 1)], 12: [(z_send, 1)]}

    def pool(i, carry):
        for at, steps in events.items():

            @pl.when(i == at)
            def _(steps=steps):
                for act, q in steps:
                    act(q)

        n, j = i // 2, i % 2
        r, after = partner(n)[0], partner(n + 1)[0]
        for s in range(2):
            slot = 2 * j + s
            refill(r, slot, s).wait()
            for u in range(examples):
                picked = [tab[pl.ds(window[s, k, u], 1), :] for k in range(8)]
                while len(picked) > 1:
                    picked = [picked[m] + picked[m + 1] for m in range(0, len(picked), 2)]
                bags[s * examples + u : s * examples + u + 1, :] = picked[0]

            @pl.when(i < 15)
            def _(s=s):
                refill(r * (1 - j) + after * j, (2 + s) * (1 - j) + s * j, s).start()

        for s in range(2):
            pooled[r, 2 * j + s, :, :] = bags[s * examples : (s + 1) * examples, :].astype(BF16)

        @pl.when((j == 1) & (n < 7))
        def _():
            bags_to(n).start()

        return carry

    lax.fori_loop(0, 16, pool, 0)
    sent = [bags_to(n) for n in range(7)]
    sent.append(pltpu.make_async_copy(pooled.at[0], arrived.at[pl.ds(t * 4, 4)], e_s.at[0]))
    sent[7].start()
    y_send(0)
    y_send(1)
    total = ys[0, :, :].astype(F32)
    for d in (4, 2, 6, 3, 5, 1, 7):
        along_y(d).wait_recv()
        total = total + yr[d - 1, :, :].astype(F32)
    total = total * (1.0 / math.sqrt(examples * X * Y * Z * 2))
    turned[...] = jnp.transpose(jnp.concatenate([total, jnp.zeros((128 - total.shape[0], 128), F32)], axis=0))
    gup_v[...] = turned[pl.ds(pl.multiple_of(yh * 32, 32), 32), 0:per_z]
    gdown_v[...] = turned[pl.ds(pl.multiple_of(yh * 32, 32), 32), per_z : 2 * per_z]
    outs = [
        pltpu.make_async_copy(gup_v, gup_hbm, ld_sem.at[0]),
        pltpu.make_async_copy(gdown_v, gdown_hbm, ld_sem.at[1]),
    ]
    for out in outs:
        out.start()

    for copy in sent[:7]:
        copy.wait_recv()
        copy.wait_send()
    for r in range(1, 8):
        ids_copy(r).wait_send()
    for q in range(2):
        for j in range(4):
            pair(j, q).wait_send()
        for k in range(2):
            for copy in (relay, direct, summed):
                copy(q, k).wait_send()
        for d in FAR:
            along_z(q, d).wait_send()
    for d in range(1, Y):
        along_y(d).wait_send()
    sent[7].wait()
    for out in outs:
        out.wait()


def finish(slot_ref, arrived_hbm, gup_in, gdown_in, emb_hbm, gup_hbm, gdown_hbm, emb_v, gup_v, gdown_v, sem):
    feats = slot_ref.shape[0]
    small = [
        (pltpu.make_async_copy(src, mid, sem.at[n]), pltpu.make_async_copy(mid, dst, sem.at[n]))
        for n, (src, mid, dst) in enumerate(((gup_in, gup_v, gup_hbm), (gdown_in, gdown_v, gdown_hbm)))
    ]
    for first, _ in small:
        first.start()
    halves = ((0, feats // 2), (feats // 2, feats))
    picks = [
        [
            pltpu.make_async_copy(
                arrived_hbm.at[slot_ref[f]], emb_v.at[:, f * 128 : (f + 1) * 128], sem.at[2 + f]
            )
            for f in range(lo, hi)
        ]
        for lo, hi in halves
    ]
    for half in picks:
        for pick in half:
            pick.start()
    outs = []
    for first, second in small:
        first.wait()
        second.start()
        outs.append(second)
    for n, (lo, hi) in enumerate(halves):
        for pick in picks[n]:
            pick.wait()
        cols = slice(lo * 128, hi * 128)
        outs.append(pltpu.make_async_copy(emb_v.at[:, cols], emb_hbm.at[:, cols], sem.at[2 + feats + n]))
        outs[-1].start()
    for out in outs:
        out.wait()


def on_device(
    next_ids, next_lengths, slot_of_table, tables, cross_input, cotangent, up_weight, down_weight
):
    examples, entries = next_ids.shape
    feats = slot_of_table.shape[0]
    slots, rows_each, embed = tables.shape
    width = cross_input.shape[1]
    rank = up_weight.shape[0]
    per_y = width // X // YL
    per_z = per_y // Z
    anywhere = pl.BlockSpec(memory_space=pl.ANY)
    vmem, dma = pltpu.VMEM, pltpu.SemaphoreType.DMA
    grads = (jax.ShapeDtypeStruct((32, per_z), F32), jax.ShapeDtypeStruct((32, per_z), F32))
    arrived, gup, gdown = pl.pallas_call(
        kernel,
        out_shape=(jax.ShapeDtypeStruct((32, examples, embed), BF16), *grads),
        in_specs=[anywhere] * 8,
        out_specs=(anywhere,) * 3,
        scratch_shapes=[
            vmem((examples, entries), jnp.int32),
            vmem((feats, examples), jnp.int32),
            vmem((1, feats), jnp.int32),
            vmem((8, 16, examples), jnp.int32),
            vmem((8, 16, examples), jnp.int32),
            vmem((8, 4, 8, examples), jnp.int32),
            pltpu.SMEM((2, 8, examples), jnp.int32),
            vmem((slots * rows_each, embed), BF16),
            vmem((slots * rows_each + 8, embed), F32),
            vmem((examples, width), BF16),
            vmem((examples, width), BF16),
            vmem((rank, width), BF16),
            vmem((width, rank), BF16),
            vmem((examples, width), BF16),
            vmem((examples, rank), BF16),
            vmem((examples, rank), BF16),
            vmem((2, width, 128), BF16),
            vmem((2, width, 128), BF16),
            vmem((2, width, 128), F32),
            vmem((2, width, 128), BF16),
            vmem((2, 2, per_y, 128), BF16),
            vmem((2, 2, per_y, 128), BF16),
            vmem((2, 2, per_y, 128), BF16),
            vmem((2, 2, per_y, 128), BF16),
            vmem((2, per_y, 128), F32),
            vmem((2, Z, 80, 128), BF16),
            vmem((2, Z - 1, 80, 128), BF16),
            vmem((2, 80, 128), BF16),
            vmem((Y - 1, 80, 128), BF16),
            vmem((128, 128), F32),
            vmem((32, per_z), F32),
            vmem((32, per_z), F32),
            vmem((2 * examples, embed), F32),
            vmem((8, 4, examples, embed), BF16),
            dma((8,)),
            dma((2,)),
            dma((8,)),
            dma((8,)),
            dma((8,)),
            dma((8,)),
            dma((4,)),
            dma((4,)),
            dma((4,)),
            dma((4,)),
            dma((4,)),
            dma((4,)),
            dma((2 * Z,)),
            dma((2 * Z,)),
            dma((Y,)),
            dma((Y,)),
            dma((8,)),
            dma((8,)),
        ],
        compiler_params=pltpu.CompilerParams(
            collective_id=0, has_side_effects=True, vmem_limit_bytes=60 * 2**20
        ),
    )(
        next_ids,
        next_lengths.T,
        slot_of_table.reshape(1, feats),
        tables.reshape(slots * rows_each, embed),
        cross_input,
        cotangent,
        up_weight,
        down_weight,
    )
    emb, gup, gdown = pl.pallas_call(
        finish,
        out_shape=(jax.ShapeDtypeStruct((examples, feats * embed), BF16), *grads),
        in_specs=[pl.BlockSpec(memory_space=pltpu.SMEM)] + [anywhere] * 3,
        out_specs=(anywhere,) * 3,
        scratch_shapes=[
            vmem((examples, feats * embed), BF16),
            vmem((32, per_z), F32),
            vmem((32, per_z), F32),
            dma((feats + 4,)),
        ],
    )(slot_of_table, arrived, gup, gdown)
    return emb, gup, gdown.T


def solution(mesh):
    return jax.shard_map(
        on_device,
        mesh=mesh,
        in_specs=(
            P(("grp", "tbl"), None),
            P(("grp", "tbl"), None),
            P(),
            P("tbl", None, None),
            P(("grp", "tbl"), None),
            P(("grp", "tbl"), None),
            P(),
            P(),
        ),
        out_specs=(P(("grp", "tbl"), None), P("tbl", "grp"), P("grp", "tbl")),
        check_vma=False,
    )
```

time: 83.8 us -> 60.1 us (0.72)
  the two profiles are of different devices: /device:TPU:7 before, /device:TPU:8 now
where the time goes in v2:
time: 60.1 us; the launch traced here: 59.9 us
  Pallas kernels  59.3 us (99%)
  between operations  0.64 us (1%)
    pallas_call x1, Pallas kernels, on_device(): pl.pallas_call(kernel, out_shape=(jax.ShapeDtypeStruct((32, examples, emb...  56.5 us
    pallas_call x1, Pallas kernels, on_device(): pl.pallas_call(finish, out_shape=(jax.ShapeDtypeStruct((examples, feats *...  2.81 us

profile of v2, /device:TPU:8, one launch (start us, length us, event | category | flops | bytes accessed | tf_op | source)
XLA Modules:
  0.0 59.9 jit_solution(1951073543008074801)
XLA Ops:
  0.6 56.5 %shard_map.103 = (bf16[32,128,128]{2,1,0:T(8,128)(2,1)}, f32[32,36]{1,0:T(8,128)}, f32[32,36]{1,0:T(8,128)}) custom-call(s32[128,256]{1,0:T(8,128)} %ids_hbm.1, s32[26,128]{1,0:T(8,128)} %bitcast.5, s32[1,26]{1,0:T(1,128)} %bitcast.6, bf16[24576,128]{1,0:T(8,128)(2,1)} %bitcast.4, bf16[128,3456]{1,0:T(8,128)(2,1)} %x_hbm.1, bf16[128,3456]{1,0:T(8,128)(2,1)} %c_hbm.1, ...), custom_call_target="tpu_custom_call" | custom-call | tf_op jit(solution)/shard_map/pallas_call | solution.py:467
  57.1 2.8 %shard_map.104 = (bf16[128,3328]{1,0:T(8,128)(2,1)}, f32[32,36]{1,0:T(8,128)}, f32[32,36]{1,0:T(8,128)}) custom-call(s32[26]{0:T(128)} %slot_ref.1, bf16[32,128,128]{2,1,0:T(8,128)(2,1)} %get-tuple-element.9.arrived_hbm, f32[32,36]{1,0:T(8,128)} %get-tuple-element.10.gup_in, f32[32,36]{1,0:T(8,128)} %get-tuple-element.11.gdown_in), custom_call_target="tpu_custom_call" | custom-call | tf_op jit(solution)/shard_map/pallas_call | solution.py:539
